TPU v7x, 32 devices: a whole 2x2x4 slice. The times are simulated.
32 devices in a mesh: grp: 2 (over x), seq: 4 (over y, core), head: 4 (over z).
Axes of the slice: x: 2, y: 2, z: 4, core: 2. Of those that a mesh axis runs over, the one named last changes fastest.
Arguments:
- q_latent: bfloat16 [8, 128, 512], P(('grp', 'seq'), 'head'), parts along dimension 0, may hold values from -6 to 6
- q_rope: bfloat16 [8, 128, 64], P(('grp', 'seq'), 'head'), parts along dimension 0, may hold values from -6 to 6
- cache_latent: bfloat16 [1152, 128, 512], P(('grp', 'seq', 'head')), parts along dimension 0, may hold values from -6 to 6
- cache_rope: bfloat16 [1152, 64, 128], P(('grp', 'seq', 'head')), parts along dimension 0, may hold values from -6 to 6
- page_table: int32 [8, 224], P(('grp', 'seq')), parts along dimension 0, may hold values from -1 to 575, as said below
- lengths: int32 [8], P(('grp', 'seq')), parts along dimension 0, may hold values from 1 to 28672, as said below
Outputs:
- attended: bfloat16 [8, 128, 512], P(('grp', 'seq'), 'head'), parts along dimension 0
There are 2 independent parts, one for each index of `grp`. A program takes and returns all parts, laid end to end along the dimension named above; each array names one. Nothing has to cross between parts.
Inputs may be any that keep to these rules, and one draw needn't show every extreme that they name: `page_table`: row s holds the pool slots of the pages of sequence s in page order; entries from ceil(lengths[s] / 128) on are -1; no slot appears twice in the table. Slots d * 36 to (d + 1) * 36 - 1 belong to device d of seq+head (seq index first). One device holds at most 14 pages of one sequence; one sequence has exactly 14 pages on every device. Sequence s has ceil(lengths[s] / 128) pages; the sequence with 14 pages on every device has length 28672.
All inputs are finite; a program needn't handle non-finite values.
Results may differ from a plain program's by a relative error of at most 0.007.
Values may be sent and summed in bfloat16 or wider, within the bound.
A program may use at most 64 MiB of HBM per device.

v0:
```python
import jax
import jax.numpy as jnp
from jax import lax
from jax.sharding import PartitionSpec as P

softmax_scale = 0.13528
floor_score = -1e30


def passed_along(array, axis, by):
    devices = lax.axis_size(axis)
    return lax.ppermute(array, axis, [(i, (i + by) % devices) for i in range(devices)])


def merge_sources(source_tops, source_totals, source_mixed):
    best_top = jnp.max(source_tops, axis=0)
    factor = jnp.exp(source_tops - best_top[None])
    total_sum = jnp.sum(factor * source_totals, axis=0)
    mixed_sum = jnp.sum(factor[..., None] * source_mixed, axis=0)
    return (mixed_sum / total_sum[..., None]).astype(jnp.bfloat16)


def on_device(q_latent, q_rope, cache_latent, cache_rope, page_table, lengths):
    slot_count, page_len, lat_width = cache_latent.shape
    seq_count = lax.axis_size("seq")
    group_count = lax.axis_size("head")
    seq_index = lax.axis_index("seq")
    head_index = lax.axis_index("head")
    tables, all_lengths = (
        lax.all_gather(page_table, "seq", axis=0, tiled=True),
        lax.all_gather(lengths, "seq", axis=0, tiled=True),
    )
    row_width = tables.shape[1]
    head_lat, head_rot = (
        lax.all_gather(q_latent, "head", axis=1, tiled=True),
        lax.all_gather(q_rope, "head", axis=1, tiled=True),
    )
    head_count = head_lat.shape[1]
    first_slot = (seq_index * group_count + head_index) * slot_count
    slot_ids = first_slot + jnp.arange(slot_count, dtype=jnp.int32)
    entry_ids = jnp.arange(seq_count * row_width, dtype=jnp.int32)
    matched = jnp.sum(
        jnp.where(tables.reshape(1, -1) == slot_ids[:, None], entry_ids[None, :] + 1, 0), axis=1
    )
    occupied = matched > 0
    entry_of = jnp.maximum(matched - 1, 0)
    slot_owner = entry_of // row_width
    page_number = entry_of % row_width
    seq_ids = jnp.arange(seq_count, dtype=jnp.int32)
    owner_hits = slot_owner[:, None] == seq_ids[None, :]
    owner_length = jnp.sum(jnp.where(owner_hits, all_lengths[None, :], 0), axis=1)
    position = page_number[:, None] * page_len + jnp.arange(page_len, dtype=jnp.int32)[None, :]
    token_live = occupied[:, None] & (position < owner_length[:, None])
    share_pages = slot_count // (seq_count + 1)
    window = 2 * share_pages
    owner_key = jnp.where(occupied, slot_owner, seq_count)
    slot_order = jnp.argsort(owner_key)
    slot_order = jnp.concatenate([slot_order, jnp.zeros((window,), jnp.int32)])
    seq_pages = jnp.sum((owner_hits & occupied[:, None]).astype(jnp.int32), axis=0)
    seq_starts = jnp.cumsum(seq_pages) - seq_pages
    window_steps = jnp.arange(window, dtype=jnp.int32)

    def visit(turn, carry):
        lat_query, rot_query, old_top, old_total, old_mixed = carry
        source = (seq_index - turn) % seq_count
        start_at = jnp.sum(jnp.where(seq_ids == source, seq_starts, 0))
        held = jnp.sum(jnp.where(seq_ids == source, seq_pages, 0))
        window_slots = lax.dynamic_slice_in_dim(slot_order, start_at, window)
        usable = (window_steps < held)[:, None] & token_live[window_slots]
        lat_pages = cache_latent[window_slots]
        rot_pages = cache_rope[window_slots]
        scores = jnp.einsum(
            "hd,btd->hbt", lat_query[0], lat_pages, preferred_element_type=jnp.float32
        )
        scores = scores + jnp.einsum(
            "he,bet->hbt", rot_query[0], rot_pages, preferred_element_type=jnp.float32
        )
        scores = jnp.where(usable[None], scores * softmax_scale, floor_score)
        new_top = jnp.maximum(old_top, jnp.max(scores, axis=(1, 2)))
        weight = jnp.where(usable[None], jnp.exp(scores - new_top[:, None, None]), 0.0)
        factor = jnp.exp(old_top - new_top)
        new_total = old_total * factor + jnp.sum(weight, axis=(1, 2))
        new_mixed = old_mixed * factor[:, None] + jnp.einsum(
            "hbt,btd->hd",
            weight.astype(jnp.bfloat16),
            lat_pages,
            preferred_element_type=jnp.float32,
        )
        lat_query, rot_query = passed_along((lat_query, rot_query), "seq", 1)
        new_top, new_total, new_mixed = passed_along((new_top, new_total, new_mixed), "seq", 1)
        return (lat_query, rot_query, new_top, new_total, new_mixed)

    start_state = (
        head_lat,
        head_rot,
        jnp.full((head_count,), floor_score, jnp.float32),
        jnp.zeros((head_count,), jnp.float32),
        jnp.zeros((head_count, lat_width), jnp.float32),
    )
    finished = lax.fori_loop(0, seq_count, visit, start_state)
    source_tops, source_totals, source_mixed = (
        lax.all_to_all(
            finished[2].reshape(1, 1, head_count), "head", split_axis=2, concat_axis=0, tiled=True
        ),
        lax.all_to_all(
            finished[3].reshape(1, 1, head_count), "head", split_axis=2, concat_axis=0, tiled=True
        ),
        lax.all_to_all(
            finished[4].reshape(1, 1, head_count, lat_width),
            "head",
            split_axis=2,
            concat_axis=0,
            tiled=True,
        ),
    )
    return merge_sources(source_tops, source_totals, source_mixed)


def solution(mesh):
    placed = (
        P(("grp", "seq"), "head", None),
        P(("grp", "seq"), "head", None),
        P(("grp", "seq", "head"), None, None),
        P(("grp", "seq", "head"), None, None),
        P(("grp", "seq"), None),
        P(("grp", "seq")),
    )
    return jax.shard_map(
        on_device,
        mesh=mesh,
        in_specs=placed,
        out_specs=P(("grp", "seq"), "head", None),
        check_vma=False,
    )
```

profile of v0, /device:TPU:0, one launch (start us, length us, event | category | flops | bytes accessed | tf_op | source)
XLA Modules:
  0.0 150.7 jit_solution(2047801408956978442)
XLA Ops:
  0.0 6.3 %all-gather = s32[4,1,224]{2,1,0:T(1,128)S(1)} all-gather(s32[1,1,224]{2,1,0:T(1,128)} %bitcast.50), channel_id=1, replica_groups=mesh['grp'=2,'seq'=4,'head'=4] {'seq'}, dimensions={0}, use_global_device_ids=true | all-gather | bytes 4480 | tf_op jit(solution)/shard_map/all_gather | solution.py:30
  9.3 5.4 %all-reduce.1 = s32[4]{0:T(128)S(1)} all-reduce(s32[4]{0:T(128)S(1)} %dynamic-update-slice), channel_id=1, replica_groups=mesh['grp'=2,'seq'=4,'head'=4] {'seq'}, use_global_device_ids=true, to_apply=%add.1 | all-reduce | flops 4 | bytes 32
  15.0 2.0 %sort.17 = (s32[36]{0:T(128)}, s32[36]{0:T(128)S(1)}) sort(s32[36]{0:T(128)S(1)} %get-tuple-element.481, s32[36]{0:T(128)S(1)} %iota.31), dimensions={0}, to_apply=%region_3.4 | sort | flops 216 | bytes 576 | tf_op jit(solution)/shard_map/jit(argsort)/sort | solution.py:57
  17.1 13.8 %all_gather.12 = bf16[1,128,512]{2,1,0:T(8,128)(2,1)S(1)} all-gather(bf16[1,32,512]{2,1,0:T(8,128)(2,1)} %param.8), channel_id=1, replica_groups=mesh['grp'=2,'seq'=4,'head'=4] {'head'}, dimensions={1}, use_global_device_ids=true | all-gather | bytes 163840 | tf_op jit(solution)/shard_map/all_gather | solution.py:35
  30.8 13.3 %all_gather.13 = bf16[1,128,64]{2,1,0:T(8,128)(2,1)S(1)} all-gather(bf16[1,32,64]{2,1,0:T(8,128)(2,1)} %param.9), channel_id=1, replica_groups=mesh['grp'=2,'seq'=4,'head'=4] {'head'}, dimensions={1}, use_global_device_ids=true | all-gather | bytes 20480 | tf_op jit(solution)/shard_map/all_gather | solution.py:36
  44.3 75.0 %while.24 = (s32[]{:T(128)}, bf16[1,128,512]{2,1,0:T(8,128)(2,1)S(1)}, bf16[1,128,64]{1,2,0:T(8,128)(2,1)S(1)}, f32[128]{0:T(128)S(1)}, f32[128]{0:T(128)S(1)}, ...) while((s32[]{:T(128)}, ...), condition=%wide.region_10.11_spmd.clone, body=%wide.region_5.10_spmd.clone.sunk | while | flops 501564000 | bytes 15254524 | solution.py:100
  47.0 3.0 %gather_fusion = bf16[14,128,512]{2,1,0:T(8,128)(2,1)S(1)} fusion(bf16[36,128,512]{2,1,0:T(8,128)(2,1)} %get-tuple-element.641, s32[1024]{0:T(1024)S(1)} %pad_clamp_fusion.2), kind=kCustom, calls=%fused_computation.1.clone.clone.1 | custom fusion | bytes 3670072 | tf_op jit(solution)/shard_map/while/body/eval_jaxpr/gather | solution.py:70
  50.1 1.7 %gather_fusion.1 = bf16[14,64,128]{2,1,0:T(8,128)(2,1)S(1)} fusion(bf16[36,64,128]{2,1,0:T(8,128)(2,1)} %get-tuple-element.642, s32[1024]{0:T(1024)S(1)} %pad_clamp_fusion.2), kind=kCustom, calls=%fused_computation.2.clone.clone.1 | custom fusion | bytes 458808 | tf_op jit(solution)/shard_map/while/body/eval_jaxpr/gather | solution.py:71
  57.9 5.1 %collective-permute-done.2 = f32[128]{0:T(128)S(1)} collective-permute-done((f32[128]{0:T(128)S(1)}, f32[128]{0:T(128)S(1)}, u32[]{:S(2)}, u32[]{:S(2)}) %collective-permute-start.2) | collective-permute-done | bytes 544 | tf_op jit(solution)/shard_map/while/body/eval_jaxpr/ppermute | solution.py:12
  65.8 3.0 %gather_fusion = bf16[14,128,512]{2,1,0:T(8,128)(2,1)S(1)} fusion(bf16[36,128,512]{2,1,0:T(8,128)(2,1)} %get-tuple-element.641, s32[1024]{0:T(1024)S(1)} %pad_clamp_fusion.2), kind=kCustom, calls=%fused_computation.1.clone.clone.1 | custom fusion | bytes 3670072 | tf_op jit(solution)/shard_map/while/body/eval_jaxpr/gather | solution.py:70
  68.8 1.7 %gather_fusion.1 = bf16[14,64,128]{2,1,0:T(8,128)(2,1)S(1)} fusion(bf16[36,64,128]{2,1,0:T(8,128)(2,1)} %get-tuple-element.642, s32[1024]{0:T(1024)S(1)} %pad_clamp_fusion.2), kind=kCustom, calls=%fused_computation.2.clone.clone.1 | custom fusion | bytes 458808 | tf_op jit(solution)/shard_map/while/body/eval_jaxpr/gather | solution.py:71
  76.7 5.1 %collective-permute-done.2 = f32[128]{0:T(128)S(1)} collective-permute-done((f32[128]{0:T(128)S(1)}, f32[128]{0:T(128)S(1)}, u32[]{:S(2)}, u32[]{:S(2)}) %collective-permute-start.2) | collective-permute-done | bytes 544 | tf_op jit(solution)/shard_map/while/body/eval_jaxpr/ppermute | solution.py:12
  84.5 3.0 %gather_fusion = bf16[14,128,512]{2,1,0:T(8,128)(2,1)S(1)} fusion(bf16[36,128,512]{2,1,0:T(8,128)(2,1)} %get-tuple-element.641, s32[1024]{0:T(1024)S(1)} %pad_clamp_fusion.2), kind=kCustom, calls=%fused_computation.1.clone.clone.1 | custom fusion | bytes 3670072 | tf_op jit(solution)/shard_map/while/body/eval_jaxpr/gather | solution.py:70
  87.5 1.7 %gather_fusion.1 = bf16[14,64,128]{2,1,0:T(8,128)(2,1)S(1)} fusion(bf16[36,64,128]{2,1,0:T(8,128)(2,1)} %get-tuple-element.642, s32[1024]{0:T(1024)S(1)} %pad_clamp_fusion.2), kind=kCustom, calls=%fused_computation.2.clone.clone.1 | custom fusion | bytes 458808 | tf_op jit(solution)/shard_map/while/body/eval_jaxpr/gather | solution.py:71
  95.4 5.1 %collective-permute-done.2 = f32[128]{0:T(128)S(1)} collective-permute-done((f32[128]{0:T(128)S(1)}, f32[128]{0:T(128)S(1)}, u32[]{:S(2)}, u32[]{:S(2)}) %collective-permute-start.2) | collective-permute-done | bytes 544 | tf_op jit(solution)/shard_map/while/body/eval_jaxpr/ppermute | solution.py:12
  103.3 3.0 %gather_fusion = bf16[14,128,512]{2,1,0:T(8,128)(2,1)S(1)} fusion(bf16[36,128,512]{2,1,0:T(8,128)(2,1)} %get-tuple-element.641, s32[1024]{0:T(1024)S(1)} %pad_clamp_fusion.2), kind=kCustom, calls=%fused_computation.1.clone.clone.1 | custom fusion | bytes 3670072 | tf_op jit(solution)/shard_map/while/body/eval_jaxpr/gather | solution.py:70
  106.3 1.7 %gather_fusion.1 = bf16[14,64,128]{2,1,0:T(8,128)(2,1)S(1)} fusion(bf16[36,64,128]{2,1,0:T(8,128)(2,1)} %get-tuple-element.642, s32[1024]{0:T(1024)S(1)} %pad_clamp_fusion.2), kind=kCustom, calls=%fused_computation.2.clone.clone.1 | custom fusion | bytes 458808 | tf_op jit(solution)/shard_map/while/body/eval_jaxpr/gather | solution.py:71
  114.1 5.1 %collective-permute-done.2 = f32[128]{0:T(128)S(1)} collective-permute-done((f32[128]{0:T(128)S(1)}, f32[128]{0:T(128)S(1)}, u32[]{:S(2)}, u32[]{:S(2)}) %collective-permute-start.2) | collective-permute-done | bytes 544 | tf_op jit(solution)/shard_map/while/body/eval_jaxpr/ppermute | solution.py:12
  120.0 4.7 %all-to-all-start = ((f32[1,1,128]{1,0,2:T(1,128)}), f32[1,1,128]{1,0,2:T(1,128)S(1)}, u32[]{:S(2)}, u32[]{:S(2)}) async-start(f32[1,1,128]{1,0,2:T(1,128)} %copy.19), calls=%async_computation | async-start | bytes 131072 | tf_op jit(solution)/shard_map/all_to_all | solution.py:102
  125.5 5.0 %all-to-all-done = f32[1,1,128]{1,0,2:T(1,128)S(1)} async-done(((f32[1,1,128]{1,0,2:T(1,128)}), f32[1,1,128]{1,0,2:T(1,128)S(1)}, u32[]{:S(2)}, u32[]{:S(2)}) %all-to-all-start) | async-done | bytes 544 | tf_op jit(solution)/shard_map/all_to_all | solution.py:102
  130.5 3.3 %all-to-all-start.2 = ((f32[1,1,128]{1,0,2:T(1,128)}), f32[1,1,128]{1,0,2:T(1,128)S(1)}, u32[]{:S(2)}, u32[]{:S(2)}) async-start(f32[1,1,128]{1,0,2:T(1,128)} %copy.20), calls=%async_computation.2 | async-start | bytes 131072 | tf_op jit(solution)/shard_map/all_to_all | solution.py:105
  134.7 4.8 %all-to-all-done.2 = f32[1,1,128]{1,0,2:T(1,128)S(1)} async-done(((f32[1,1,128]{1,0,2:T(1,128)}), f32[1,1,128]{1,0,2:T(1,128)S(1)}, u32[]{:S(2)}, u32[]{:S(2)}) %all-to-all-start.2) | async-done | bytes 544 | tf_op jit(solution)/shard_map/all_to_all | solution.py:105
  139.5 3.4 %all-to-all-start.1 = ((f32[1,1,128,512]{3,1,0,2:T(1,128)}), f32[1,1,128,512]{3,1,0,2:T(1,128)S(1)}, u32[]{:S(2)}, u32[]{:S(2)}) async-start(f32[1,1,128,512]{3,1,0,2:T(1,128)} %reshape.237), calls=%async_computation.1 | async-start | bytes 524288 | tf_op jit(solution)/shard_map/all_to_all | solution.py:108
  145.3 4.4 %all-to-all-done.1 = f32[1,1,128,512]{3,1,0,2:T(1,128)S(1)} async-done(((f32[1,1,128,512]{3,1,0,2:T(1,128)}), f32[1,1,128,512]{3,1,0,2:T(1,128)S(1)}, u32[]{:S(2)}, u32[]{:S(2)}) %all-to-all-start.1) | async-done | bytes 262176 | tf_op jit(solution)/shard_map/all_to_all | solution.py:108
  (128 shorter events, 36.1 us)
Async XLA Ops:
  55.5 7.5 %collective-permute-start.4 = (f32[128,512]{1,0:T(8,128)S(1)}, f32[128,512]{1,0:T(8,128)S(1)}, u32[]{:S(2)}, u32[]{:S(2)}) collective-permute-start(f32[128,512]{1,0:T(8,128)S(1)} %fusion.51), channel_id=1, source_target_pairs={{0,4},{4,8},{8,12},{12,0},{1,5},{5,9},{9,13},{13,1},{2,6},{6,10},{... | collective-permute-start | bytes 786440 | tf_op jit(solution)/shard_map/while/body/eval_jaxpr/ppermute | solution.py:12
  55.6 7.5 %collective-permute-start = (bf16[1,128,512]{2,1,0:T(8,128)(2,1)S(1)}, bf16[1,128,512]{2,1,0:T(8,128)(2,1)S(1)}, u32[]{:S(2)}, u32[]{:S(2)}) collective-permute-start(bf16[1,128,512]{2,1,0:T(8,128)(2,1)S(1)} %copy.30), channel_id=1, source_target_pairs={{0,4},{4,8},{8,12},{12,0},{1,5},{5,9},{9,13},{13,1},{2,6},{6,10},{... | collective-permute-start | bytes 393224 | tf_op jit(solution)/shard_map/while/body/eval_jaxpr/ppermute | solution.py:12
  56.6 6.5 %collective-permute-start.1 = (bf16[1,128,64]{1,2,0:T(8,128)(2,1)S(1)}, bf16[1,128,64]{1,2,0:T(8,128)(2,1)S(1)}, u32[]{:S(2)}, u32[]{:S(2)}) collective-permute-start(bf16[1,128,64]{1,2,0:T(8,128)(2,1)S(1)} %copy.31), channel_id=1, source_target_pairs={{0,4},{4,8},{8,12},{12,0},{1,5},{5,9},{9,13},{13,1},{2,6},{6,10},{... | collective-permute-start | bytes 49160 | tf_op jit(solution)/shard_map/while/body/eval_jaxpr/ppermute | solution.py:12
  56.6 6.4 %collective-permute-start.2 = (f32[128]{0:T(128)S(1)}, f32[128]{0:T(128)S(1)}, u32[]{:S(2)}, u32[]{:S(2)}) collective-permute-start(f32[128]{0:T(128)S(1)} %max.29), channel_id=1, source_target_pairs={{0,4},{4,8},{8,12},{12,0},{1,5},{5,9},{9,13},{13,1},{2,6},{6,10},{... | collective-permute-start | bytes 1544 | tf_op jit(solution)/shard_map/while/body/eval_jaxpr/ppermute | solution.py:12
  57.9 5.2 %collective-permute-start.3 = (f32[128]{0:T(128)S(1)}, f32[128]{0:T(128)S(1)}, u32[]{:S(2)}, u32[]{:S(2)}) collective-permute-start(f32[128]{0:T(128)S(1)} %get-tuple-element.589), channel_id=1, source_target_pairs={{0,4},{4,8},{8,12},{12,0},{1,5},{5,9},{9,13},{13,1},{2,6},{6,10},{... | collective-permute-start | bytes 1544 | tf_op jit(solution)/shard_map/while/body/eval_jaxpr/ppermute | solution.py:12
  74.3 7.5 %collective-permute-start.4 = (f32[128,512]{1,0:T(8,128)S(1)}, f32[128,512]{1,0:T(8,128)S(1)}, u32[]{:S(2)}, u32[]{:S(2)}) collective-permute-start(f32[128,512]{1,0:T(8,128)S(1)} %fusion.51), channel_id=1, source_target_pairs={{0,4},{4,8},{8,12},{12,0},{1,5},{5,9},{9,13},{13,1},{2,6},{6,10},{... | collective-permute-start | bytes 786440 | tf_op jit(solution)/shard_map/while/body/eval_jaxpr/ppermute | solution.py:12
  74.3 7.5 %collective-permute-start = (bf16[1,128,512]{2,1,0:T(8,128)(2,1)S(1)}, bf16[1,128,512]{2,1,0:T(8,128)(2,1)S(1)}, u32[]{:S(2)}, u32[]{:S(2)}) collective-permute-start(bf16[1,128,512]{2,1,0:T(8,128)(2,1)S(1)} %copy.30), channel_id=1, source_target_pairs={{0,4},{4,8},{8,12},{12,0},{1,5},{5,9},{9,13},{13,1},{2,6},{6,10},{... | collective-permute-start | bytes 393224 | tf_op jit(solution)/shard_map/while/body/eval_jaxpr/ppermute | solution.py:12
  75.3 6.5 %collective-permute-start.1 = (bf16[1,128,64]{1,2,0:T(8,128)(2,1)S(1)}, bf16[1,128,64]{1,2,0:T(8,128)(2,1)S(1)}, u32[]{:S(2)}, u32[]{:S(2)}) collective-permute-start(bf16[1,128,64]{1,2,0:T(8,128)(2,1)S(1)} %copy.31), channel_id=1, source_target_pairs={{0,4},{4,8},{8,12},{12,0},{1,5},{5,9},{9,13},{13,1},{2,6},{6,10},{... | collective-permute-start | bytes 49160 | tf_op jit(solution)/shard_map/while/body/eval_jaxpr/ppermute | solution.py:12
  75.4 6.4 %collective-permute-start.2 = (f32[128]{0:T(128)S(1)}, f32[128]{0:T(128)S(1)}, u32[]{:S(2)}, u32[]{:S(2)}) collective-permute-start(f32[128]{0:T(128)S(1)} %max.29), channel_id=1, source_target_pairs={{0,4},{4,8},{8,12},{12,0},{1,5},{5,9},{9,13},{13,1},{2,6},{6,10},{... | collective-permute-start | bytes 1544 | tf_op jit(solution)/shard_map/while/body/eval_jaxpr/ppermute | solution.py:12
  76.6 5.2 %collective-permute-start.3 = (f32[128]{0:T(128)S(1)}, f32[128]{0:T(128)S(1)}, u32[]{:S(2)}, u32[]{:S(2)}) collective-permute-start(f32[128]{0:T(128)S(1)} %get-tuple-element.589), channel_id=1, source_target_pairs={{0,4},{4,8},{8,12},{12,0},{1,5},{5,9},{9,13},{13,1},{2,6},{6,10},{... | collective-permute-start | bytes 1544 | tf_op jit(solution)/shard_map/while/body/eval_jaxpr/ppermute | solution.py:12
  93.0 7.5 %collective-permute-start.4 = (f32[128,512]{1,0:T(8,128)S(1)}, f32[128,512]{1,0:T(8,128)S(1)}, u32[]{:S(2)}, u32[]{:S(2)}) collective-permute-start(f32[128,512]{1,0:T(8,128)S(1)} %fusion.51), channel_id=1, source_target_pairs={{0,4},{4,8},{8,12},{12,0},{1,5},{5,9},{9,13},{13,1},{2,6},{6,10},{... | collective-permute-start | bytes 786440 | tf_op jit(solution)/shard_map/while/body/eval_jaxpr/ppermute | solution.py:12
  93.1 7.5 %collective-permute-start = (bf16[1,128,512]{2,1,0:T(8,128)(2,1)S(1)}, bf16[1,128,512]{2,1,0:T(8,128)(2,1)S(1)}, u32[]{:S(2)}, u32[]{:S(2)}) collective-permute-start(bf16[1,128,512]{2,1,0:T(8,128)(2,1)S(1)} %copy.30), channel_id=1, source_target_pairs={{0,4},{4,8},{8,12},{12,0},{1,5},{5,9},{9,13},{13,1},{2,6},{6,10},{... | collective-permute-start | bytes 393224 | tf_op jit(solution)/shard_map/while/body/eval_jaxpr/ppermute | solution.py:12
  94.1 6.5 %collective-permute-start.1 = (bf16[1,128,64]{1,2,0:T(8,128)(2,1)S(1)}, bf16[1,128,64]{1,2,0:T(8,128)(2,1)S(1)}, u32[]{:S(2)}, u32[]{:S(2)}) collective-permute-start(bf16[1,128,64]{1,2,0:T(8,128)(2,1)S(1)} %copy.31), channel_id=1, source_target_pairs={{0,4},{4,8},{8,12},{12,0},{1,5},{5,9},{9,13},{13,1},{2,6},{6,10},{... | collective-permute-start | bytes 49160 | tf_op jit(solution)/shard_map/while/body/eval_jaxpr/ppermute | solution.py:12
  94.1 6.4 %collective-permute-start.2 = (f32[128]{0:T(128)S(1)}, f32[128]{0:T(128)S(1)}, u32[]{:S(2)}, u32[]{:S(2)}) collective-permute-start(f32[128]{0:T(128)S(1)} %max.29), channel_id=1, source_target_pairs={{0,4},{4,8},{8,12},{12,0},{1,5},{5,9},{9,13},{13,1},{2,6},{6,10},{... | collective-permute-start | bytes 1544 | tf_op jit(solution)/shard_map/while/body/eval_jaxpr/ppermute | solution.py:12
  95.3 5.2 %collective-permute-start.3 = (f32[128]{0:T(128)S(1)}, f32[128]{0:T(128)S(1)}, u32[]{:S(2)}, u32[]{:S(2)}) collective-permute-start(f32[128]{0:T(128)S(1)} %get-tuple-element.589), channel_id=1, source_target_pairs={{0,4},{4,8},{8,12},{12,0},{1,5},{5,9},{9,13},{13,1},{2,6},{6,10},{... | collective-permute-start | bytes 1544 | tf_op jit(solution)/shard_map/while/body/eval_jaxpr/ppermute | solution.py:12
  111.8 7.5 %collective-permute-start.4 = (f32[128,512]{1,0:T(8,128)S(1)}, f32[128,512]{1,0:T(8,128)S(1)}, u32[]{:S(2)}, u32[]{:S(2)}) collective-permute-start(f32[128,512]{1,0:T(8,128)S(1)} %fusion.51), channel_id=1, source_target_pairs={{0,4},{4,8},{8,12},{12,0},{1,5},{5,9},{9,13},{13,1},{2,6},{6,10},{... | collective-permute-start | bytes 786440 | tf_op jit(solution)/shard_map/while/body/eval_jaxpr/ppermute | solution.py:12
  111.8 7.5 %collective-permute-start = (bf16[1,128,512]{2,1,0:T(8,128)(2,1)S(1)}, bf16[1,128,512]{2,1,0:T(8,128)(2,1)S(1)}, u32[]{:S(2)}, u32[]{:S(2)}) collective-permute-start(bf16[1,128,512]{2,1,0:T(8,128)(2,1)S(1)} %copy.30), channel_id=1, source_target_pairs={{0,4},{4,8},{8,12},{12,0},{1,5},{5,9},{9,13},{13,1},{2,6},{6,10},{... | collective-permute-start | bytes 393224 | tf_op jit(solution)/shard_map/while/body/eval_jaxpr/ppermute | solution.py:12
  112.8 6.5 %collective-permute-start.1 = (bf16[1,128,64]{1,2,0:T(8,128)(2,1)S(1)}, bf16[1,128,64]{1,2,0:T(8,128)(2,1)S(1)}, u32[]{:S(2)}, u32[]{:S(2)}) collective-permute-start(bf16[1,128,64]{1,2,0:T(8,128)(2,1)S(1)} %copy.31), channel_id=1, source_target_pairs={{0,4},{4,8},{8,12},{12,0},{1,5},{5,9},{9,13},{13,1},{2,6},{6,10},{... | collective-permute-start | bytes 49160 | tf_op jit(solution)/shard_map/while/body/eval_jaxpr/ppermute | solution.py:12
  112.9 6.4 %collective-permute-start.2 = (f32[128]{0:T(128)S(1)}, f32[128]{0:T(128)S(1)}, u32[]{:S(2)}, u32[]{:S(2)}) collective-permute-start(f32[128]{0:T(128)S(1)} %max.29), channel_id=1, source_target_pairs={{0,4},{4,8},{8,12},{12,0},{1,5},{5,9},{9,13},{13,1},{2,6},{6,10},{... | collective-permute-start | bytes 1544 | tf_op jit(solution)/shard_map/while/body/eval_jaxpr/ppermute | solution.py:12
  114.1 5.2 %collective-permute-start.3 = (f32[128]{0:T(128)S(1)}, f32[128]{0:T(128)S(1)}, u32[]{:S(2)}, u32[]{:S(2)}) collective-permute-start(f32[128]{0:T(128)S(1)} %get-tuple-element.589), channel_id=1, source_target_pairs={{0,4},{4,8},{8,12},{12,0},{1,5},{5,9},{9,13},{13,1},{2,6},{6,10},{... | collective-permute-start | bytes 1544 | tf_op jit(solution)/shard_map/while/body/eval_jaxpr/ppermute | solution.py:12
  120.0 10.5 %all-to-all-start = ((f32[1,1,128]{1,0,2:T(1,128)}), f32[1,1,128]{1,0,2:T(1,128)S(1)}, u32[]{:S(2)}, u32[]{:S(2)}) async-start(f32[1,1,128]{1,0,2:T(1,128)} %copy.19), calls=%async_computation | async-start | bytes 131072 | tf_op jit(solution)/shard_map/all_to_all | solution.py:102
  130.5 9.0 %all-to-all-start.2 = ((f32[1,1,128]{1,0,2:T(1,128)}), f32[1,1,128]{1,0,2:T(1,128)S(1)}, u32[]{:S(2)}, u32[]{:S(2)}) async-start(f32[1,1,128]{1,0,2:T(1,128)} %copy.20), calls=%async_computation.2 | async-start | bytes 131072 | tf_op jit(solution)/shard_map/all_to_all | solution.py:105
  139.5 10.2 %all-to-all-start.1 = ((f32[1,1,128,512]{3,1,0,2:T(1,128)}), f32[1,1,128,512]{3,1,0,2:T(1,128)S(1)}, u32[]{:S(2)}, u32[]{:S(2)}) async-start(f32[1,1,128,512]{3,1,0,2:T(1,128)} %reshape.237), calls=%async_computation.1 | async-start | bytes 524288 | tf_op jit(solution)/shard_map/all_to_all | solution.py:108
where the time goes:
time: 152 us; the launch traced here: 151 us
  blocking collectives  38.8 us (26%)
  waiting for transfers between devices  34.8 us (23%)
  local copies, waits for them, and re-layouts  25.8 us (17%)
  starting transfers between devices  20.9 us (14%)
  other arithmetic  13 us (9%)
  matrix products  8.55 us (6%)
  loops' own time  8.14 us (5%)
    ppermute x20, waiting for transfers between devices, passed_along(): lax.ppermute(array, axis, [(i, (i + by) % devices) for i in range(devices)])  20.6 us
    all_gather x1, blocking collectives, on_device(): lax.all_gather(q_latent, 'head', axis=1, tiled=True)  13.8 us
    all_gather x1, blocking collectives, on_device(): lax.all_gather(q_rope, 'head', axis=1, tiled=True)  13.3 us
    gather x4, local copies, waits for them, and re-layouts, visit(): lat_pages = cache_latent[window_slots]  12 us
    ppermute x20, starting transfers between devices, passed_along(): lax.ppermute(array, axis, [(i, (i + by) % devices) for i in range(devices)])  9.47 us
    another operation x1, loops' own time, on_device(): finished = lax.fori_loop(0, seq_count, visit, start_state)  8.14 us
    gather x4, local copies, waits for them, and re-layouts, visit(): rot_pages = cache_rope[window_slots]  6.62 us
    all_gather x1, blocking collectives, on_device(): lax.all_gather(page_table, 'seq', axis=0, tiled=True)  6.32 us
  transfers between devices with their start and end apart: 23, of which 7 were waited for; matrix products, arithmetic and copies ran while one was open for 2% of the time, Pallas kernels for 0%

commit v1 on v0

v1 whole, which is shorter than its diff:
```python
import functools

import jax
import jax.numpy as jnp
from jax import lax
from jax.experimental import pallas as pl
from jax.experimental.pallas import tpu as pltpu
from jax.sharding import PartitionSpec as P

MESH = pl.DeviceIdType.MESH
softmax_scale = 0.13528
floor_score = -1e30
F32 = jnp.float32
BF16 = jnp.bfloat16


def swapped(index, by):
    out, bit = index, 1
    while bit <= by:
        if by & bit:
            out = out + bit - 2 * bit * ((index // bit) % 2)
        bit *= 2
    return out


def kernel(
    n_s, n_h, window,
    ql, qr, kc, kr, tab, lens, out,
    kc_v, kr_v, ql_all, qr_all, tab_all, len_all, plan_v, plan_s, sc, acc, acc_m, acc_l,
    send_c, recv_c, send_y, recv_y, send_z, recv_z,
    cache_sem, plan_sem, tab_ss, tab_rs, q_ss, q_rs, c_ss, c_rs, y_ss, y_rs, z_ss, z_rs,
):
    s, h = lax.axis_index("seq"), lax.axis_index("head")
    y_count = n_s // 2
    slots, page, lat = kc.shape
    rows = ql.shape[1]
    heads = n_h * rows
    width = tab.shape[1]

    cache_copies = [
        pltpu.make_async_copy(kc, kc_v, cache_sem.at[0]),
        pltpu.make_async_copy(kr, kr_v, cache_sem.at[1]),
    ]
    for copy in cache_copies:
        copy.start()

    barrier = pltpu.get_barrier_semaphore()
    for d in range(1, n_s):
        pl.semaphore_signal(barrier, inc=1, device_id={"seq": swapped(s, d)}, device_id_type=MESH)
    for d in range(1, n_h):
        pl.semaphore_signal(barrier, inc=1, device_id={"head": swapped(h, d)}, device_id_type=MESH)
    pl.semaphore_wait(barrier, n_s + n_h - 2)

    sends = []

    def remote(src, dst, ss, rs, target):
        copy = pltpu.make_async_remote_copy(
            src_ref=src, dst_ref=dst, send_sem=ss, recv_sem=rs, device_id=target, device_id_type=MESH
        )
        copy.start()
        sends.append(copy)

    for d in range(1, n_s):
        target = {"seq": swapped(s, d)}
        remote(tab, tab_all.at[s], tab_ss.at[0, d], tab_rs.at[0, s], target)
        remote(lens, len_all.at[s], tab_ss.at[1, d], tab_rs.at[1, s], target)

    send_at = [0]

    def push(lat_src, rot_src, seq_slot, head_slot, target):
        i = send_at[0]
        send_at[0] += 1
        remote(lat_src, ql_all.at[seq_slot, head_slot], q_ss.at[0, i], q_rs.at[0, seq_slot, head_slot], target)
        remote(rot_src, qr_all.at[seq_slot, head_slot], q_ss.at[1, i], q_rs.at[1, seq_slot, head_slot], target)

    def landed(seq_slot, head_slot):
        for i, ref in enumerate((ql_all, qr_all)):
            at = ref.at[seq_slot, head_slot]
            pltpu.make_async_copy(at, at, q_rs.at[i, seq_slot, head_slot]).wait()

    for d in range(n_h - 1, 0, -1):
        push(ql.at[0], qr.at[0], s, h, {"head": swapped(h, d)})
    for k in range(1, y_count):
        push(ql.at[0], qr.at[0], s, h, {"seq": swapped(s, 2 * k)})
    push(ql.at[0], qr.at[0], s, h, {"seq": swapped(s, 1)})
    ql_all[s, h] = ql[0]
    qr_all[s, h] = qr[0]
    tab_all[s] = tab[...]
    len_all[s] = lens[...]

    for d in range(1, n_s):
        other = swapped(s, d)
        for i, ref in enumerate((tab_all, len_all)):
            at = ref.at[other]
            pltpu.make_async_copy(at, at, tab_rs.at[i, other]).wait()
    tables = tab_all[...].reshape(n_s, width)
    all_lens = len_all[...].reshape(n_s, 128)[:, :1]
    local = tables - (s * n_h + h) * slots
    hit = (local >= 0) & (local < slots) & (tables >= 0)
    before = lax.broadcasted_iota(jnp.int32, (width, width), 0) < lax.broadcasted_iota(jnp.int32, (width, width), 1)
    rank = jnp.dot(
        hit.astype(F32).astype(BF16), before.astype(F32).astype(BF16), preferred_element_type=F32
    ).astype(jnp.int32)
    page_no = lax.broadcasted_iota(jnp.int32, (n_s, width), 1)
    limit = jnp.clip(all_lens - page_no * page, 0, page)
    lane = lax.broadcasted_iota(jnp.int32, (n_s, 128), 1)
    slot_plan = jnp.zeros((n_s, 128), jnp.int32)
    limit_plan = jnp.zeros((n_s, 128), jnp.int32)
    for j in range(window):
        chosen = hit & (rank == j)
        slot_j = jnp.sum(jnp.where(chosen, local, 0), axis=1, keepdims=True)
        limit_j = jnp.sum(jnp.where(chosen, limit, 0), axis=1, keepdims=True)
        slot_plan = jnp.where(lane == j, slot_j, slot_plan)
        limit_plan = jnp.where(lane == j, limit_j, limit_plan)
    plan_v[0] = slot_plan
    plan_v[1] = limit_plan

    for d in range(1, n_h):
        g = swapped(h, d)
        landed(s, g)
        for k in range(1, y_count):
            push(ql_all.at[s, g], qr_all.at[s, g], s, g, {"seq": swapped(s, 2 * k)})
        push(ql_all.at[s, g], qr_all.at[s, g], s, g, {"seq": swapped(s, 1)})

    plan_copy = pltpu.make_async_copy(plan_v, plan_s, plan_sem.at[0])
    plan_copy.start()
    plan_copy.wait()
    for copy in cache_copies:
        copy.wait()

    group = 2 if window % 2 == 0 else 1
    steps = window // group
    span = group * page
    tokens = lax.broadcasted_iota(jnp.int32, (heads, page), 1)

    def attend(seq_slot):
        lat_q = ql_all[seq_slot].reshape(heads, lat)
        rot_q = qr_all[seq_slot].reshape(heads, qr.shape[2])
        best = None
        for p in range(steps):
            held = [plan_s[0, seq_slot, p * group + i] for i in range(group)]
            keys = jnp.concatenate([kc_v[i] for i in held], axis=0)
            rot = jnp.concatenate([kr_v[i] for i in held], axis=1)
            scores = lax.dot_general(lat_q, keys, (((1,), (1,)), ((), ())), preferred_element_type=F32)
            scores = scores + jnp.dot(rot_q, rot, preferred_element_type=F32)
            live = jnp.concatenate(
                [tokens < plan_s[1, seq_slot, p * group + i] for i in range(group)], axis=1
            )
            scores = jnp.where(live, scores * softmax_scale, floor_score)
            sc[p] = scores
            best = scores if best is None else jnp.maximum(best, scores)
        top = jnp.max(best, axis=1, keepdims=True).astype(BF16).astype(F32)
        shift = jnp.where(top > 0.1 * floor_score, top, 0.0)
        total = None
        for p in range(steps):
            held = [plan_s[0, seq_slot, p * group + i] for i in range(group)]
            keys = jnp.concatenate([kc_v[i] for i in held], axis=0)
            weight = jnp.exp(sc[p] - shift)
            total = weight if total is None else total + weight
            part = jnp.dot(weight.astype(BF16), keys, preferred_element_type=F32)
            if p == 0:
                acc[...] = part
            else:
                acc[...] += part
        return top, jnp.sum(total, axis=1, keepdims=True)

    def packed(mixed, top, total):
        high = total.astype(BF16)
        low = (total - high.astype(F32)).astype(BF16)
        at = lax.broadcasted_iota(jnp.int32, (mixed.shape[0], 128), 1)
        stats = jnp.where(at == 0, top, jnp.where(at == 1, high.astype(F32), low.astype(F32)))
        return jnp.concatenate([mixed.astype(BF16), stats.astype(BF16)], axis=1)

    def unpacked(block):
        mixed = block[:, :lat].astype(F32)
        stats = block[:, lat:].astype(F32)
        return mixed, stats[:, 0:1], stats[:, 1:2] + stats[:, 2:3]

    def merged(states):
        top = functools.reduce(jnp.maximum, [state[1] for state in states])
        mixed, total = 0.0, 0.0
        for part_mixed, part_top, part_total in states:
            factor = jnp.exp(part_top - top)
            mixed = mixed + factor * part_mixed
            total = total + factor * part_total
        return mixed, top, total

    def own_part(k):
        top, total = attend(swapped(s, 2 * k))
        acc_m[k] = acc[...]
        acc_l[0, k] = jnp.broadcast_to(top, (heads, 128))
        acc_l[1, k] = jnp.broadcast_to(total, (heads, 128))

    def partner_part(k):
        top, total = attend(swapped(s, 2 * k + 1))
        send_c[k] = packed(acc[...], top, total)
        remote(send_c.at[k], recv_c.at[k], c_ss.at[k], c_rs.at[k], {"seq": swapped(s, 1)})

    own_part(0)
    for k in range(1, y_count):
        other = swapped(s, 2 * k)
        for d in range(n_h):
            g = swapped(h, d)
            landed(other, g)
            push(ql_all.at[other, g], qr_all.at[other, g], other, g, {"seq": swapped(s, 1)})
    for k in range(y_count):
        other = swapped(s, 2 * k + 1)
        for d in range(n_h):
            landed(other, swapped(h, d))
        partner_part(k)
        if k > 0:
            own_part(k)

    def group_state(k, g):
        at = pl.ds(pl.multiple_of(g * rows, rows), rows)
        mine = (acc_m[k, at, :], acc_l[0, k, at, :][:, :1], acc_l[1, k, at, :][:, :1])
        theirs = unpacked(recv_c[k, at, :])
        return [mine, theirs]

    def wait_block(ref, sem):
        pltpu.make_async_copy(ref, ref, sem).wait()

    order = list(range(n_h - 1, -1, -1))
    for k in range(1, y_count):
        wait_block(recv_c.at[k], c_rs.at[k])
        for d in order:
            g = swapped(h, d)
            send_y[k - 1, d] = packed(*merged(group_state(k, g)))
            remote(
                send_y.at[k - 1, d], recv_y.at[k - 1, d], y_ss.at[k - 1, d], y_rs.at[k - 1, d],
                {"seq": swapped(s, 2 * k)},
            )
    wait_block(recv_c.at[0], c_rs.at[0])
    final = None
    for d in order:
        states = group_state(0, swapped(h, d))
        for k in range(1, y_count):
            wait_block(recv_y.at[k - 1, d], y_rs.at[k - 1, d])
            states.append(unpacked(recv_y[k - 1, d]))
        state = merged(states)
        if d > 0:
            send_z[d - 1] = packed(*state)
            remote(
                send_z.at[d - 1], recv_z.at[d - 1], z_ss.at[d - 1], z_rs.at[d - 1],
                {"head": swapped(h, d)},
            )
        else:
            final = [state]
    for d in range(1, n_h):
        wait_block(recv_z.at[d - 1], z_rs.at[d - 1])
        final.append(unpacked(recv_z[d - 1]))
    mixed, _, total = merged(final)
    out[0] = (mixed / total).astype(BF16)
    for copy in sends:
        copy.wait_send()


def solution(mesh):
    n_s, n_h = mesh.shape["seq"], mesh.shape["head"]

    def on_device(q_latent, q_rope, cache_latent, cache_rope, page_table, lengths):
        slots, page, lat = cache_latent.shape
        rot = cache_rope.shape[1]
        rows = q_latent.shape[1]
        heads = rows * n_h
        width = page_table.shape[1]
        window = width // (n_s * n_h)
        y_count = n_s // 2
        group = 2 if window % 2 == 0 else 1
        pack = lat + 128
        dma = pltpu.SemaphoreType.DMA
        others = max(y_count - 1, 1)
        pushes = (n_h - 1) + n_h * y_count + n_h * (y_count - 1)
        vmem = pl.BlockSpec(memory_space=pltpu.VMEM)
        anyspace = pl.BlockSpec(memory_space=pl.ANY)
        padded = jnp.broadcast_to(lengths.reshape(1, 1), (1, 128))
        return pl.pallas_call(
            functools.partial(kernel, n_s, n_h, window),
            out_shape=jax.ShapeDtypeStruct((1, rows, lat), BF16),
            in_specs=[vmem, vmem, anyspace, anyspace, vmem, vmem],
            out_specs=vmem,
            scratch_shapes=[
                pltpu.VMEM((slots, page, lat), BF16),
                pltpu.VMEM((slots, rot, page), BF16),
                pltpu.VMEM((n_s, n_h, rows, lat), BF16),
                pltpu.VMEM((n_s, n_h, rows, rot), BF16),
                pltpu.VMEM((n_s, 1, width), jnp.int32),
                pltpu.VMEM((n_s, 1, 128), jnp.int32),
                pltpu.VMEM((2, n_s, 128), jnp.int32),
                pltpu.SMEM((2, n_s, 128), jnp.int32),
                pltpu.VMEM((window // group, heads, group * page), F32),
                pltpu.VMEM((heads, lat), F32),
                pltpu.VMEM((y_count, heads, lat), F32),
                pltpu.VMEM((2, y_count, heads, 128), F32),
                pltpu.VMEM((y_count, heads, pack), BF16),
                pltpu.VMEM((y_count, heads, pack), BF16),
                pltpu.VMEM((others, n_h, rows, pack), BF16),
                pltpu.VMEM((others, n_h, rows, pack), BF16),
                pltpu.VMEM((n_h - 1, rows, pack), BF16),
                pltpu.VMEM((n_h - 1, rows, pack), BF16),
                dma((2,)),
                dma((1,)),
                dma((2, n_s)),
                dma((2, n_s)),
                dma((2, pushes)),
                dma((2, n_s, n_h)),
                dma((y_count,)),
                dma((y_count,)),
                dma((others, n_h)),
                dma((others, n_h)),
                dma((n_h - 1,)),
                dma((n_h - 1,)),
            ],
            compiler_params=pltpu.CompilerParams(
                collective_id=0, has_side_effects=True, vmem_limit_bytes=48 * 1024 * 1024
            ),
        )(q_latent, q_rope, cache_latent, cache_rope, page_table, padded)

    placed = (
        P(("grp", "seq"), "head", None),
        P(("grp", "seq"), "head", None),
        P(("grp", "seq", "head"), None, None),
        P(("grp", "seq", "head"), None, None),
        P(("grp", "seq"), None),
        P(("grp", "seq")),
    )
    return jax.shard_map(
        on_device,
        mesh=mesh,
        in_specs=placed,
        out_specs=P(("grp", "seq"), "head", None),
        check_vma=False,
    )
```

time: 152 us -> 36 us (0.24)
  blocking collectives: 38.8 us -> 0 us
  waiting for transfers between devices: 34.8 us -> 0 us
  Pallas kernels: 0 us -> 28.8 us
  starting transfers between devices: 20.9 us -> 0 us
  local copies, waits for them, and re-layouts: 25.8 us -> 6.15 us
  other arithmetic: 13 us -> 0 us
  matrix products: 8.55 us -> 0 us
  loops' own time: 8.14 us -> 0 us
    all_gather x3 -> x0, blocking collectives: 33.4 us -> none  [the longest x1 13.8 us: on_device(): lax.all_gather(q_latent, 'head', axis=1, tiled=True)]
    pallas_call x0 -> x1, Pallas kernels: none -> 28.8 us  [on_device(): pl.pallas_call(functools.partial(kernel, n_s, n_h, window), out_shape=jax...]
    gather x12 -> x0, local copies, waits for them, and re-layouts: 20.9 us -> none  [the longest x4 12 us: visit(): lat_pages = cache_latent[window_slots]]
    ppermute x20 -> x0, waiting for transfers between devices: 20.6 us -> none  [passed_along(): lax.ppermute(array, axis, [(i, (i + by) % devices) for i in range(devices)])]
    all_to_all x3 -> x0, waiting for transfers between devices: 14.2 us -> none  [the longest x1 5.02 us: on_device(): lax.all_to_all(finished[2].reshape(1, 1, head_count), 'head', split_axis=...]
    all_to_all x3 -> x0, starting transfers between devices: 11.4 us -> none  [the longest x1 4.73 us: on_device(): lax.all_to_all(finished[2].reshape(1, 1, head_count), 'head', split_axis=...]
    ppermute x20 -> x0, starting transfers between devices: 9.47 us -> none  [passed_along(): lax.ppermute(array, axis, [(i, (i + by) % devices) for i in range(devices)])]
    dot_general x12 -> x0, matrix products: 8.55 us -> none  [the longest x4 3.39 us: visit(): jnp.einsum('hbt,btd->hd', weight.astype(jnp.bfloat16), lat_pages, preferr...]
  transfers between devices with their start and end apart: 23 -> 0, of which waited for: 7 -> 0; matrix products, arithmetic and copies ran while one was open for 2% -> 0% of each run, Pallas kernels for 0% -> 0%
where the time goes in v1:
time: 36 us; the launch traced here: 35.6 us
  Pallas kernels  28.8 us (80%)
  local copies, waits for them, and re-layouts  6.15 us (17%)
  between operations  0.68 us (2%)
    pallas_call x1, Pallas kernels, on_device(): pl.pallas_call(functools.partial(kernel, n_s, n_h, window), out_shape=jax...  28.8 us
    unnamed x11, local copies, waits for them, and re-layouts  6.15 us

profile of v1, /device:TPU:0, one launch (start us, length us, event | category | flops | bytes accessed | tf_op | source)
XLA Modules:
  0.0 35.6 jit_solution(9656363177605781755)
XLA Ops:
  0.7 0.0 copy-start
  0.7 2.3 %copy-done = bf16[36,128,512]{2,1,0:T(8,128)(2,1)S(1)} copy-done((bf16[36,128,512]{2,1,0:T(8,128)(2,1)S(1)}, bf16[36,128,512]{2,1,0:T(8,128)(2,1)}, u32[]{:S(2)}) %copy-start) | copy-done | bytes 4718616
  3.0 0.0 copy-start.1
  3.0 1.1 %copy-done.1 = bf16[36,64,128]{2,1,0:T(8,128)(2,1)S(1)} copy-done((bf16[36,64,128]{2,1,0:T(8,128)(2,1)S(1)}, bf16[36,64,128]{2,1,0:T(8,128)(2,1)}, u32[]{:S(2)}) %copy-start.1) | copy-done | bytes 589848
  4.1 0.0 copy-start.2
  4.1 0.8 %copy-done.2 = bf16[1,32,512]{2,1,0:T(8,128)(2,1)S(1)} copy-done((bf16[1,32,512]{2,1,0:T(8,128)(2,1)S(1)}, bf16[1,32,512]{2,1,0:T(8,128)(2,1)}, u32[]{:S(2)}) %copy-start.2) | copy-done | bytes 32792
  4.8 0.0 copy-start.3
  4.8 0.7 %copy-done.3 = bf16[1,32,64]{2,1,0:T(8,128)(2,1)S(1)} copy-done((bf16[1,32,64]{2,1,0:T(8,128)(2,1)S(1)}, bf16[1,32,64]{2,1,0:T(8,128)(2,1)}, u32[]{:S(2)}) %copy-start.3) | copy-done | bytes 4120
  5.5 0.0 copy-start.4
  5.5 0.7 %copy-done.4 = s32[1,224]{1,0:T(1,128)S(1)} copy-done((s32[1,224]{1,0:T(1,128)S(1)}, s32[1,224]{1,0:T(1,128)}, u32[]{:S(2)}) %copy-start.4) | copy-done | bytes 920
  6.2 28.8 %shard_map.64 = bf16[1,32,512]{2,1,0:T(8,128)(2,1)S(1)} custom-call(bf16[1,32,512]{2,1,0:T(8,128)(2,1)S(1)} %copy-done.2, bf16[1,32,64]{2,1,0:T(8,128)(2,1)S(1)} %copy-done.3, bf16[36,128,512]{2,1,0:T(8,128)(2,1)S(1)} %copy-done, bf16[36,64,128]{2,1,0:T(8,128)(2,1)S(1)} %copy-done.1, s32[1,224]{1,0:T(1,128)S(1)} %copy-done.4, s32[1,128]{1,0:T(1,128)S(1)} %broadcast_in_dim.8.lens), custom_call_target="tpu_custom_call" | custom-call | tf_op jit(solution)/shard_map/pallas_call | solution.py:277
  35.0 0.6 %copy.9 = bf16[1,32,512]{2,1,0:T(8,128)(2,1)} copy(bf16[1,32,512]{2,1,0:T(8,128)(2,1)S(1)} %shard_map.64) | data formatting | bytes 65536
  (1 shorter events, 0.0 us)
Async XLA Ops:
  0.7 2.3 %copy-start = (bf16[36,128,512]{2,1,0:T(8,128)(2,1)S(1)}, bf16[36,128,512]{2,1,0:T(8,128)(2,1)}, u32[]{:S(2)}) copy-start(bf16[36,128,512]{2,1,0:T(8,128)(2,1)} %kc.1) | copy-start | bytes 14155780
  3.0 1.1 %copy-start.1 = (bf16[36,64,128]{2,1,0:T(8,128)(2,1)S(1)}, bf16[36,64,128]{2,1,0:T(8,128)(2,1)}, u32[]{:S(2)}) copy-start(bf16[36,64,128]{2,1,0:T(8,128)(2,1)} %kr.1) | copy-start | bytes 1769476
  4.1 0.8 %copy-start.2 = (bf16[1,32,512]{2,1,0:T(8,128)(2,1)S(1)}, bf16[1,32,512]{2,1,0:T(8,128)(2,1)}, u32[]{:S(2)}) copy-start(bf16[1,32,512]{2,1,0:T(8,128)(2,1)} %ql.1) | copy-start | bytes 98308
  4.8 0.7 %copy-start.3 = (bf16[1,32,64]{2,1,0:T(8,128)(2,1)S(1)}, bf16[1,32,64]{2,1,0:T(8,128)(2,1)}, u32[]{:S(2)}) copy-start(bf16[1,32,64]{2,1,0:T(8,128)(2,1)} %qr.1) | copy-start | bytes 12292
  5.5 0.7 %copy-start.4 = (s32[1,224]{1,0:T(1,128)S(1)}, s32[1,224]{1,0:T(1,128)}, u32[]{:S(2)}) copy-start(s32[1,224]{1,0:T(1,128)} %tab.1) | copy-start | bytes 2692

commit v2 on v1

--- a/solution.py
+++ b/solution.py
@@ -26,9 +26,9 @@
 def kernel(
     n_s, n_h, window,
     ql, qr, kc, kr, tab, lens, out,
-    kc_v, kr_v, ql_all, qr_all, tab_all, len_all, plan_v, plan_s, sc, acc, acc_m, acc_l,
+    kc_v, kr_v, ql_all, qr_all, tab_all, len_all, plan_v, plan_s, sc, weights, acc, acc_m, acc_l,
     send_c, recv_c, send_y, recv_y, send_z, recv_z,
-    cache_sem, plan_sem, tab_ss, tab_rs, q_ss, q_rs, c_ss, c_rs, y_ss, y_rs, z_ss, z_rs,
+    cache_sem, own_sem, plan_sem, tab_ss, tab_rs, q_ss, q_rs, c_ss, c_rs, y_ss, y_rs, z_ss, z_rs,
 ):
     s, h = lax.axis_index("seq"), lax.axis_index("head")
     y_count = n_s // 2
@@ -41,7 +41,12 @@
         pltpu.make_async_copy(kc, kc_v, cache_sem.at[0]),
         pltpu.make_async_copy(kr, kr_v, cache_sem.at[1]),
     ]
-    for copy in cache_copies:
+    own_copies = [
+        pltpu.make_async_copy(tab, tab_all.at[s], own_sem.at[0]),
+        pltpu.make_async_copy(ql.at[0], ql_all.at[s, h], own_sem.at[1]),
+        pltpu.make_async_copy(qr.at[0], qr_all.at[s, h], own_sem.at[2]),
+    ]
+    for copy in own_copies + cache_copies:
         copy.start()
 
     barrier = pltpu.get_barrier_semaphore()
@@ -49,6 +54,9 @@
         pl.semaphore_signal(barrier, inc=1, device_id={"seq": swapped(s, d)}, device_id_type=MESH)
     for d in range(1, n_h):
         pl.semaphore_signal(barrier, inc=1, device_id={"head": swapped(h, d)}, device_id_type=MESH)
+    len_all[s] = lens[...]
+    for copy in own_copies:
+        copy.wait()
     pl.semaphore_wait(barrier, n_s + n_h - 2)
 
     sends = []
@@ -62,7 +70,7 @@
 
     for d in range(1, n_s):
         target = {"seq": swapped(s, d)}
-        remote(tab, tab_all.at[s], tab_ss.at[0, d], tab_rs.at[0, s], target)
+        remote(tab_all.at[s], tab_all.at[s], tab_ss.at[0, d], tab_rs.at[0, s], target)
         remote(lens, len_all.at[s], tab_ss.at[1, d], tab_rs.at[1, s], target)
 
     send_at = [0]
@@ -79,14 +87,10 @@
             pltpu.make_async_copy(at, at, q_rs.at[i, seq_slot, head_slot]).wait()
 
     for d in range(n_h - 1, 0, -1):
-        push(ql.at[0], qr.at[0], s, h, {"head": swapped(h, d)})
+        push(ql_all.at[s, h], qr_all.at[s, h], s, h, {"head": swapped(h, d)})
     for k in range(1, y_count):
-        push(ql.at[0], qr.at[0], s, h, {"seq": swapped(s, 2 * k)})
-    push(ql.at[0], qr.at[0], s, h, {"seq": swapped(s, 1)})
-    ql_all[s, h] = ql[0]
-    qr_all[s, h] = qr[0]
-    tab_all[s] = tab[...]
-    len_all[s] = lens[...]
+        push(ql_all.at[s, h], qr_all.at[s, h], s, h, {"seq": swapped(s, 2 * k)})
+    push(ql_all.at[s, h], qr_all.at[s, h], s, h, {"seq": swapped(s, 1)})
 
     for d in range(1, n_s):
         other = swapped(s, d)
@@ -130,6 +134,7 @@
 
     group = 2 if window % 2 == 0 else 1
     steps = window // group
+    mix = window
     span = group * page
     tokens = lax.broadcasted_iota(jnp.int32, (heads, page), 1)
 
@@ -153,11 +158,12 @@
         shift = jnp.where(top > 0.1 * floor_score, top, 0.0)
         total = None
         for p in range(steps):
-            held = [plan_s[0, seq_slot, p * group + i] for i in range(group)]
-            keys = jnp.concatenate([kc_v[i] for i in held], axis=0)
             weight = jnp.exp(sc[p] - shift)
             total = weight if total is None else total + weight
-            part = jnp.dot(weight.astype(BF16), keys, preferred_element_type=F32)
+            weights[:, p * span : (p + 1) * span] = weight.astype(BF16)
+        for p in range(0, window, mix):
+            keys = jnp.concatenate([kc_v[plan_s[0, seq_slot, p + i]] for i in range(mix)], axis=0)
+            part = jnp.dot(weights[:, p * page : (p + mix) * page], keys, preferred_element_type=F32)
             if p == 0:
                 acc[...] = part
             else:
@@ -197,19 +203,21 @@
         remote(send_c.at[k], recv_c.at[k], c_ss.at[k], c_rs.at[k], {"seq": swapped(s, 1)})
 
     own_part(0)
+    for d in range(n_h):
+        landed(swapped(s, 1), swapped(h, d))
+    partner_part(0)
     for k in range(1, y_count):
         other = swapped(s, 2 * k)
         for d in range(n_h):
             g = swapped(h, d)
             landed(other, g)
             push(ql_all.at[other, g], qr_all.at[other, g], other, g, {"seq": swapped(s, 1)})
-    for k in range(y_count):
+    for k in range(1, y_count):
+        own_part(k)
         other = swapped(s, 2 * k + 1)
         for d in range(n_h):
             landed(other, swapped(h, d))
         partner_part(k)
-        if k > 0:
-            own_part(k)
 
     def group_state(k, g):
         at = pl.ds(pl.multiple_of(g * rows, rows), rows)
@@ -272,12 +280,12 @@
         others = max(y_count - 1, 1)
         pushes = (n_h - 1) + n_h * y_count + n_h * (y_count - 1)
         vmem = pl.BlockSpec(memory_space=pltpu.VMEM)
-        anyspace = pl.BlockSpec(memory_space=pl.ANY)
+        hbm = pl.BlockSpec(memory_space=pltpu.HBM)
         padded = jnp.broadcast_to(lengths.reshape(1, 1), (1, 128))
         return pl.pallas_call(
             functools.partial(kernel, n_s, n_h, window),
             out_shape=jax.ShapeDtypeStruct((1, rows, lat), BF16),
-            in_specs=[vmem, vmem, anyspace, anyspace, vmem, vmem],
+            in_specs=[hbm, hbm, hbm, hbm, hbm, vmem],
             out_specs=vmem,
             scratch_shapes=[
                 pltpu.VMEM((slots, page, lat), BF16),
@@ -289,6 +297,7 @@
                 pltpu.VMEM((2, n_s, 128), jnp.int32),
                 pltpu.SMEM((2, n_s, 128), jnp.int32),
                 pltpu.VMEM((window // group, heads, group * page), F32),
+                pltpu.VMEM((heads, window * page), BF16),
                 pltpu.VMEM((heads, lat), F32),
                 pltpu.VMEM((y_count, heads, lat), F32),
                 pltpu.VMEM((2, y_count, heads, 128), F32),
@@ -299,6 +308,7 @@
                 pltpu.VMEM((n_h - 1, rows, pack), BF16),
                 pltpu.VMEM((n_h - 1, rows, pack), BF16),
                 dma((2,)),
+                dma((3,)),
                 dma((1,)),
                 dma((2, n_s)),
                 dma((2, n_s)),
@@ -312,7 +322,7 @@
                 dma((n_h - 1,)),
             ],
             compiler_params=pltpu.CompilerParams(
-                collective_id=0, has_side_effects=True, vmem_limit_bytes=48 * 1024 * 1024
+                collective_id=0, has_side_effects=True, vmem_limit_bytes=67_043_328
             ),
         )(q_latent, q_rope, cache_latent, cache_rope, page_table, padded)
 

time: 36 us -> 32.7 us (0.908)
  local copies, waits for them, and re-layouts: 6.15 us -> 1.91 us
  Pallas kernels: 28.8 us -> 29.9 us
    unnamed x11 -> x1, local copies, waits for them, and re-layouts: 6.15 us -> 1.38 us
    pallas_call x1, Pallas kernels: 28.8 us -> 29.9 us  [on_device(): pl.pallas_call(functools.partial(kernel, n_s, n_h, window), out_shape=jax...]
    broadcast_in_dim x1, local copies, waits for them, and re-layouts: 0.01 us -> 0.54 us  [on_device(): padded = jnp.broadcast_to(lengths.reshape(1, 1), (1, 128))]
where the time goes in v2:
time: 32.7 us; the launch traced here: 32.5 us
  Pallas kernels  29.9 us (91%)
  local copies, waits for them, and re-layouts  1.91 us (6%)
  between operations  0.66 us (2%)
    pallas_call x1, Pallas kernels, on_device(): pl.pallas_call(functools.partial(kernel, n_s, n_h, window), out_shape=jax...  29.9 us
    unnamed x1, local copies, waits for them, and re-layouts  1.38 us

profile of v2, /device:TPU:0, one launch (start us, length us, event | category | flops | bytes accessed | tf_op | source)
XLA Modules:
  0.0 32.5 jit_solution(9104331519410187804)
XLA Ops:
  0.7 0.5 %broadcast_in_dim.8.lens = s32[1,128]{1,0:T(1,128)} broadcast(s32[]{:T(128)} %bitcast.1), dimensions={} | broadcast | bytes 516 | tf_op jit(solution)/shard_map/broadcast_in_dim | solution.py:284
  1.2 29.9 %shard_map.64 = bf16[1,32,512]{2,1,0:T(8,128)(2,1)} custom-call(bf16[1,32,512]{2,1,0:T(8,128)(2,1)} %ql.1, bf16[1,32,64]{2,1,0:T(8,128)(2,1)} %qr.1, bf16[36,128,512]{2,1,0:T(8,128)(2,1)} %kc.1, bf16[36,64,128]{2,1,0:T(8,128)(2,1)} %kr.1, s32[1,224]{1,0:T(1,128)} %tab.1, s32[1,128]{1,0:T(1,128)} %broadcast_in_dim.8.lens), custom_call_target="tpu_custom_call" | custom-call | tf_op jit(solution)/shard_map/pallas_call | solution.py:285
  31.1 1.4 %copy.9 = bf16[1,32,512]{2,1,0:T(8,128)(2,1)} copy(bf16[1,32,512]{2,1,0:T(8,128)(2,1)} %shard_map.64) | data formatting | bytes 65536
